TPU v7x, 32 devices: a whole 2x2x4 slice. The times are simulated.
32 devices in a mesh: gx: 2 (over core), gy: 4 (over y, x), gz: 4 (over z).
Axes of the slice: x: 2, y: 2, z: 4, core: 2. Of those that a mesh axis runs over, the one named last changes fastest.
Arguments:
- right_side: float32 [3, 32, 64, 512], P(None, 'gx', 'gy', 'gz'), may hold values from -64 to 64
- damage: int32 [32, 64, 512], P('gx', 'gy', 'gz'), may hold values from 0 to 15
Outputs:
- displacement: float32 [3, 32, 64, 512], P(None, 'gx', 'gy', 'gz')
- norms: float32 [2], replicated
All inputs are finite; a program needn't handle non-finite values.
Results may differ from a plain program's by a relative error of at most 0.0003.
Values sent between devices are 32-bit elements; how exact they have to be, the bound alone decides.
A program may use at most 64 MiB of HBM per device.

v0:
```python
import jax
import jax.numpy as jnp
from jax import lax
from jax.sharding import PartitionSpec as P

BLOCK = 16
COARSE = 8


FLOOR_STIFFNESS = 0.05
MASS_TERM = 0.001
COUPLING = 2.5
RELAXATION = 0.6


def padded_2(block, sides, width):
    for axis, dim in sides:
        count = lax.axis_size(axis)
        forward = [(i, i + 1) for i in range(count - 1)]
        backward = [(target, source) for source, target in forward]
        low = lax.ppermute(
            lax.slice_in_dim(block, block.shape[dim] - width, None, axis=dim), axis, forward
        )
        high = lax.ppermute(lax.slice_in_dim(block, 0, width, axis=dim), axis, backward)
        block = jnp.concatenate([low, block, high], axis=dim)
    return block


def stiffness_of(damage):
    damage_level = damage.astype(jnp.float32) / 15.0
    return (1.0 - damage_level) ** 2 * (1.0 - FLOOR_STIFFNESS) + FLOOR_STIFFNESS


def diagonal_of(coefficient, mass_term):
    return coefficient * (6.0 + 2.0 * COUPLING) + mass_term


def stencil(padded, coefficient, mass_term):
    extent = (padded.shape[1] - 2, padded.shape[2] - 2, padded.shape[3] - 2)

    def neighbour(component, offset):
        return padded[
            component,
            1 + offset[0] : 1 + offset[0] + extent[0],
            1 + offset[1] : 1 + offset[1] + extent[1],
            1 + offset[2] : 1 + offset[2] + extent[2],
        ]

    def joined(first, second, factor):
        return tuple((first[number] + factor * second[number] for number in range(3)))

    unit_steps = ((1, 0, 0), (0, 1, 0), (0, 0, 1))
    images = []
    for component in range(3):
        centre = neighbour(component, (0, 0, 0))
        beside_all = jnp.zeros_like(centre)
        for partner in range(3):
            step_up = unit_steps[partner]
            step_down = joined((0, 0, 0), step_up, -1)
            beside_all = (
                beside_all + neighbour(component, step_up) + neighbour(component, step_down)
            )
        own_up = unit_steps[component]
        own_down = joined((0, 0, 0), own_up, -1)
        axial_part = 2.0 * centre - neighbour(component, own_up) - neighbour(component, own_down)
        mixed_part = jnp.zeros_like(centre)
        for partner in range(3):
            if partner != component:
                other_up = unit_steps[partner]
                mixed_part = (
                    mixed_part
                    + neighbour(partner, joined(own_up, other_up, 1))
                    - neighbour(partner, joined(own_up, other_up, -1))
                    - neighbour(partner, joined(own_down, other_up, 1))
                    + neighbour(partner, joined(own_down, other_up, -1))
                )
        images.append(
            coefficient * (6.0 * centre - beside_all + COUPLING * (axial_part - 0.25 * mixed_part))
            + mass_term * centre
        )
    return jnp.stack(images)


def crop_by(source, margin):
    return source[
        ...,
        margin : source.shape[-3] - margin,
        margin : source.shape[-2] - margin,
        margin : source.shape[-1] - margin,
    ]


def inside(margin, extent):
    position_x = (
        lax.axis_index("gx") * extent[0]
        + jnp.arange(extent[0] + 2 * margin, dtype=jnp.int32)
        - margin
    )
    position_y = (
        lax.axis_index("gy") * extent[1]
        + jnp.arange(extent[1] + 2 * margin, dtype=jnp.int32)
        - margin
    )
    position_z = (
        lax.axis_index("gz") * extent[2]
        + jnp.arange(extent[2] + 2 * margin, dtype=jnp.int32)
        - margin
    )
    flag_x = ((position_x >= 0) & (position_x < extent[0] * lax.axis_size("gx"))).astype(
        jnp.float32
    )
    flag_y = ((position_y >= 0) & (position_y < extent[1] * lax.axis_size("gy"))).astype(
        jnp.float32
    )
    flag_z = ((position_z >= 0) & (position_z < extent[2] * lax.axis_size("gz"))).astype(
        jnp.float32
    )
    return flag_x[:, None, None] * flag_y[None, :, None] * flag_z[None, None, :]


def block_sums(source):
    channels, size_x, size_y, size_z = source.shape
    return jnp.sum(
        source.reshape(
            channels, size_x // BLOCK, BLOCK, size_y // BLOCK, BLOCK, size_z // BLOCK, BLOCK
        ),
        axis=(2, 4, 6),
    )


def spread(block_field):
    channels, size_x, size_y, size_z = block_field.shape
    widened = jnp.broadcast_to(
        block_field[:, :, None, :, None, :, None],
        (channels, size_x, BLOCK, size_y, BLOCK, size_z, BLOCK),
    )
    return widened.reshape(channels, size_x * BLOCK, size_y * BLOCK, size_z * BLOCK)


def coarse_sweeps(coarse_load, mean_stiffness, padder):
    coarse_coefficient = BLOCK**2 * mean_stiffness
    coarse_mass = BLOCK**3 * MASS_TERM
    coarse_diagonal = diagonal_of(coarse_coefficient, coarse_mass)
    correction = RELAXATION * coarse_load / coarse_diagonal
    for repeat in range(COARSE - 1):
        coarse_image = stencil(padder(correction), coarse_coefficient, coarse_mass)
        correction = correction + RELAXATION * (coarse_load - coarse_image) / coarse_diagonal
    return correction


def coarse_correction(residual, coefficient):
    local_sums = jnp.concatenate(
        [block_sums(residual), block_sums(coefficient[None]) / BLOCK**3], axis=0
    )
    channels, size_x, size_y, size_z = local_sums.shape
    count_y = lax.axis_size("gy")
    count_z = lax.axis_size("gz")
    gathered = lax.all_gather(local_sums[None], ("gy", "gz"), axis=0, tiled=True)
    coarse_slab = gathered.reshape(count_y, count_z, channels, size_x, size_y, size_z)
    coarse_slab = coarse_slab.transpose(2, 3, 0, 4, 1, 5).reshape(
        channels, size_x, count_y * size_y, count_z * size_z
    )

    def padder(coarse_field):
        widened = padded_2(coarse_field, (("gx", 1),), 1)
        return jnp.pad(widened, ((0, 0), (0, 0), (1, 1), (1, 1)))

    correction = coarse_sweeps(coarse_slab[:3], coarse_slab[3], padder)
    start_x = jnp.zeros((), jnp.int32)
    own_block = lax.dynamic_slice(
        correction,
        (
            jnp.zeros((), jnp.int32),
            start_x,
            lax.axis_index("gy") * size_y,
            lax.axis_index("gz") * size_z,
        ),
        (3, size_x, size_y, size_z),
    )
    return spread(own_block)


def on_device(right_side, damage):
    coefficient = stiffness_of(damage)
    extent = coefficient.shape
    load_sum = lax.psum(jnp.sum(right_side * right_side), ("gx", "gy", "gz"))
    stacked = jnp.concatenate([right_side, coefficient[None]], axis=0)
    widened = padded_2(stacked, (("gx", 1), ("gy", 2), ("gz", 3)), 2)
    load_wide = widened[:3]
    stiff_wide = widened[3]
    diag_wide = diagonal_of(stiff_wide, MASS_TERM)
    load_loop = crop_by(load_wide, 1)
    stiff_loop = crop_by(stiff_wide, 1)
    diag_loop = crop_by(diag_wide, 1)
    loop_mask = inside(1, extent)
    first_sweep = RELAXATION * load_wide / diag_wide
    second_sweep = (
        crop_by(first_sweep, 1)
        + RELAXATION * (load_loop - stencil(first_sweep, stiff_loop, MASS_TERM)) / diag_loop
    ) * loop_mask
    residual = right_side - stencil(second_sweep, coefficient, MASS_TERM)
    displacement = crop_by(second_sweep, 1) + coarse_correction(residual, coefficient)
    deep_field = padded_2(displacement, (("gx", 1), ("gy", 2), ("gz", 3)), 3)
    third_sweep = (
        crop_by(deep_field, 1)
        + RELAXATION * (load_wide - stencil(deep_field, stiff_wide, MASS_TERM)) / diag_wide
    ) * inside(2, extent)
    fourth_sweep = (
        crop_by(third_sweep, 1)
        + RELAXATION * (load_loop - stencil(third_sweep, stiff_loop, MASS_TERM)) / diag_loop
    ) * loop_mask
    displacement = crop_by(fourth_sweep, 1)
    residual = right_side - stencil(fourth_sweep, coefficient, MASS_TERM)
    total_count = (
        3
        * extent[0]
        * extent[1]
        * extent[2]
        * lax.axis_size("gx")
        * lax.axis_size("gy")
        * lax.axis_size("gz")
    )
    residual_sum = lax.psum(jnp.sum(residual * residual), ("gx", "gy", "gz"))
    norms = jnp.stack([jnp.sqrt(load_sum / total_count), jnp.sqrt(residual_sum / total_count)])
    return (displacement, norms)


def solution(mesh):
    placed = (P(None, "gx", "gy", "gz"), P("gx", "gy", "gz"))
    return jax.shard_map(
        on_device,
        mesh=mesh,
        in_specs=placed,
        out_specs=(P(None, "gx", "gy", "gz"), P()),
        check_vma=False,
    )
```

profile of v0, /device:TPU:0, one launch (start us, length us, event | category | flops | bytes accessed | tf_op | source)
XLA Modules:
  0.0 221.1 jit_solution(12910278271885519980)
XLA Ops:
  2.5 2.4 %collective-permute-start = (f32[4,2,16,128]{3,2,1,0:T(8,128)S(1)}, f32[4,2,16,128]{3,2,1,0:T(8,128)S(1)}, u32[]{:S(2)}, u32[]{:S(2)}) collective-permute-start(f32[4,2,16,128]{3,2,1,0:T(8,128)S(1)} %get-tuple-element.22), channel_id=1, source_target_pairs={{0,16},{1,17},{2,18},{3,19},{4,20},{5,21},{6,22},{7,23},{8,24},{9,... | collective-permute-start | bytes 196616 | tf_op jit(solution)/shard_map/ppermute | solution.py:21
  4.9 1.3 collective-permute-start.1
  6.3 1.7 collective-permute-done.1
  9.2 1.3 collective-permute-start.3
  10.5 4.8 %collective-permute-start.2 = (f32[4,20,2,128]{3,0,2,1:T(4,128)S(1)}, f32[4,20,2,128]{3,0,2,1:T(4,128)S(1)}, u32[]{:S(2)}, u32[]{:S(2)}) collective-permute-start(f32[4,20,2,128]{3,0,2,1:T(4,128)S(1)} %copy.330), channel_id=1, source_target_pairs={{0,4},{4,8},{8,12},{1,5},{5,9},{9,13},{2,6},{6,10},{10,14},{3,7},{... | collective-permute-start | bytes 245768 | tf_op jit(solution)/shard_map/ppermute | solution.py:21
  20.6 4.6 %collective-permute-start.4 = (f32[4,20,20,2]{2,0,3,1:T(4,128)S(1)}, f32[4,20,20,2]{2,0,3,1:T(4,128)S(1)}, u32[]{:S(2)}, u32[]{:S(2)}) collective-permute-start(f32[4,20,20,2]{2,0,3,1:T(4,128)S(1)} %copy.314), channel_id=1, source_target_pairs={{0,1},{1,2},{2,3},{4,5},{5,6},{6,7},{8,9},{9,10},{10,11},{12,13},{... | collective-permute-start | bytes 38408 | tf_op jit(solution)/shard_map/ppermute | solution.py:21
  27.8 1.6 copy.317
  29.4 2.4 %pad_maximum_fusion = f32[4,20,20,132]{3,2,1,0:T(8,128)S(1)} fusion(f32[4,20,20,2]{3,2,1,0:T(8,128)} %copy.317, f32[4,20,2,128]{3,2,1,0:T(2,128)S(1)} %copy.313, f32[4,2,16,128]{3,2,1,0:T(8,128)} %copy-done.18, f32[1,16,16,128]{3,2,1,0:T(8,128)S(1)} %fusion.369, f32[3,16,16,128]{3,2,1,0:T(8,128)S(1)} %copy-done.2, f32[4,2,16,128]{3,2,1,0:T(8,128)} %copy-done.17, ...), kind=kLoop, calls=%fused_computation | loop fusion | flops 1478400 | bytes 1689600 | tf_op jit(solution)/shard_map/concatenate | solution.py:25
  32.7 1.6 fusion.98
  34.2 1.3 fusion.76
  35.6 1.5 multiply_add_fusion
  39.8 1.6 fusion.173
  41.5 1.3 reduce_sum.57
  42.8 1.3 reduce_sum.58
  45.2 1.9 multiply_reduce_fusion
  48.6 43.3 %all-gather = f32[64,1,1,8]{3,2,1,0:T(1,128)S(1)} all-gather(f32[4,1,1,8]{3,2,1,0:T(1,128)S(1)} %bitcast.367), channel_id=2, replica_groups=mesh['gx'=2,'gy'=4,'gz'=4] {'gy','gz'}, dimensions={0}, use_global_device_ids=true | all-gather | bytes 2176 | tf_op jit(solution)/shard_map/all_gather | solution.py:158
  93.4 1.3 collective-permute-start.6
  94.8 1.7 collective-permute-done.6
  96.8 2.1 collective-permute-start.9
  100.2 1.8 collective-permute-done.8
  102.3 2.1 collective-permute-start.11
  105.7 1.8 collective-permute-done.10
  107.8 2.1 collective-permute-start.13
  109.9 1.5 collective-permute-start.12
  111.4 1.6 collective-permute-done.12
  113.3 2.1 collective-permute-start.15
  115.4 1.3 collective-permute-start.14
  116.7 1.8 collective-permute-done.14
  118.8 2.1 collective-permute-start.17
  122.2 1.8 collective-permute-done.16
  124.4 2.1 collective-permute-start.19
  127.8 1.7 collective-permute-done.18
  130.3 2.1 collective-permute-start.20
  133.8 1.8 collective-permute-done.21
  137.0 4.6 %collective-permute-start.22 = (f32[3,22,3,128]{3,1,2,0:T(8,128)S(1)}, f32[3,22,3,128]{3,1,2,0:T(8,128)S(1)}, u32[]{:S(2)}, u32[]{:S(2)}) collective-permute-start(f32[3,22,3,128]{3,1,2,0:T(8,128)S(1)} %copy.321), channel_id=1, source_target_pairs={{0,4},{4,8},{8,12},{1,5},{5,9},{9,13},{2,6},{6,10},{10,14},{3,7},{... | collective-permute-start | bytes 304136 | tf_op jit(solution)/shard_map/ppermute | solution.py:21
  141.5 1.6 collective-permute-done.23
  145.9 2.3 %copy.325 = f32[3,22,22,3]{2,1,3,0:T(8,128)} copy(f32[3,22,22,3]{3,2,1,0:T(8,128)} %get-tuple-element.16) | data formatting | bytes 34848 | tf_op jit(solution)/shard_map/slice | solution.py:22
  150.6 5.2 %collective-permute-start.24 = (f32[3,22,22,3]{2,1,3,0:T(8,128)}, f32[3,22,22,3]{2,1,3,0:T(8,128)}, u32[]{:S(2)}, u32[]{:S(2)}) collective-permute-start(f32[3,22,22,3]{2,1,3,0:T(8,128)} %copy.325), channel_id=1, source_target_pairs={{0,1},{1,2},{2,3},{4,5},{5,6},{6,7},{8,9},{9,10},{10,11},{12,13},{... | collective-permute-start | bytes 52280 | tf_op jit(solution)/shard_map/ppermute | solution.py:21
  157.8 1.4 copy.327
  159.2 2.3 %copy.328 = f32[3,22,22,3]{3,2,1,0:T(8,128)} copy(f32[3,22,22,3]{2,1,3,0:T(8,128)} %collective-permute-done.25) | data formatting | bytes 34848 | tf_op jit(solution)/shard_map/ppermute | solution.py:24
  161.5 2.2 pad_maximum_fusion.1
  163.7 1.6 fusion.32
  165.3 1.6 fusion.23
  166.9 1.4 fusion.14
  169.3 1.6 fusion.52
  170.9 1.6 fusion.63
  172.5 1.4 fusion.41
  177.9 41.3 %all-reduce.7 = (f32[]{:T(128)}, f32[]{:T(128)}) all-reduce(f32[]{:T(128)} %fusion.108, f32[]{:T(128)} %get-tuple-element.8), channel_id=1, replica_groups=mesh['gx'=2,'gy'=4,'gz'=4] {'gx','gy','gz'}, use_global_device_ids=true, to_apply=%region_7.8 | all-reduce | flops 2 | bytes 16 | tf_op jit(solution)/shard_map/psum | solution.py:223
  (156 shorter events, 42.0 us)
Async XLA Ops:
  0.6 16.8 %copy-start.2 = (f32[3,16,16,128]{3,2,1,0:T(8,128)S(1)}, f32[3,16,16,128]{3,2,1,0:T(8,128)}, u32[]{:S(2)}) copy-start(f32[3,16,16,128]{3,2,1,0:T(8,128)} %param.2) | copy-start | bytes 1179652
  2.5 3.8 %collective-permute-start = (f32[4,2,16,128]{3,2,1,0:T(8,128)S(1)}, f32[4,2,16,128]{3,2,1,0:T(8,128)S(1)}, u32[]{:S(2)}, u32[]{:S(2)}) collective-permute-start(f32[4,2,16,128]{3,2,1,0:T(8,128)S(1)} %get-tuple-element.22), channel_id=1, source_target_pairs={{0,16},{1,17},{2,18},{3,19},{4,20},{5,21},{6,22},{7,23},{8,24},{9,... | collective-permute-start | bytes 196616 | tf_op jit(solution)/shard_map/ppermute | solution.py:21
  4.9 3.1 %collective-permute-start.1 = (f32[4,2,16,128]{3,2,1,0:T(8,128)S(1)}, f32[4,2,16,128]{3,2,1,0:T(8,128)S(1)}, u32[]{:S(2)}, u32[]{:S(2)}) collective-permute-start(f32[4,2,16,128]{3,2,1,0:T(8,128)S(1)} %get-tuple-element.23), channel_id=1, source_target_pairs={{16,0},{17,1},{18,2},{19,3},{20,4},{21,5},{22,6},{23,7},{24,8},{25... | collective-permute-start | bytes 196616 | tf_op jit(solution)/shard_map/ppermute | solution.py:24
  6.3 11.3 %copy-start.17 = (f32[4,2,16,128]{3,2,1,0:T(8,128)}, f32[4,2,16,128]{3,2,1,0:T(8,128)S(1)}, u32[]{:S(2)}) copy-start(f32[4,2,16,128]{3,2,1,0:T(8,128)S(1)} %collective-permute-done) | copy-start | bytes 196612
  8.0 9.6 %copy-start.18 = (f32[4,2,16,128]{3,2,1,0:T(8,128)}, f32[4,2,16,128]{3,2,1,0:T(8,128)S(1)}, u32[]{:S(2)}) copy-start(f32[4,2,16,128]{3,2,1,0:T(8,128)S(1)} %collective-permute-done.1) | copy-start | bytes 196612
  9.2 7.0 %collective-permute-start.3 = (f32[4,20,2,128]{3,0,2,1:T(4,128)S(1)}, f32[4,20,2,128]{3,0,2,1:T(4,128)S(1)}, u32[]{:S(2)}, u32[]{:S(2)}) collective-permute-start(f32[4,20,2,128]{3,0,2,1:T(4,128)S(1)} %copy.331), channel_id=1, source_target_pairs={{4,0},{8,4},{12,8},{5,1},{9,5},{13,9},{6,2},{10,6},{14,10},{7,3},{... | collective-permute-start | bytes 245768 | tf_op jit(solution)/shard_map/ppermute | solution.py:24
  10.5 6.9 %collective-permute-start.2 = (f32[4,20,2,128]{3,0,2,1:T(4,128)S(1)}, f32[4,20,2,128]{3,0,2,1:T(4,128)S(1)}, u32[]{:S(2)}, u32[]{:S(2)}) collective-permute-start(f32[4,20,2,128]{3,0,2,1:T(4,128)S(1)} %copy.330), channel_id=1, source_target_pairs={{0,4},{4,8},{8,12},{1,5},{5,9},{9,13},{2,6},{6,10},{10,14},{3,7},{... | collective-permute-start | bytes 245768 | tf_op jit(solution)/shard_map/ppermute | solution.py:21
  17.5 0.6 copy-start.15
  19.3 8.6 %collective-permute-start.5 = (f32[4,20,20,2]{2,0,3,1:T(4,128)S(1)}, f32[4,20,20,2]{2,0,3,1:T(4,128)S(1)}, u32[]{:S(2)}, u32[]{:S(2)}) collective-permute-start(f32[4,20,20,2]{2,0,3,1:T(4,128)S(1)} %copy.315), channel_id=1, source_target_pairs={{1,0},{2,1},{3,2},{5,4},{6,5},{7,6},{9,8},{10,9},{11,10},{13,12},{... | collective-permute-start | bytes 38408 | tf_op jit(solution)/shard_map/ppermute | solution.py:24
  20.6 6.7 %collective-permute-start.4 = (f32[4,20,20,2]{2,0,3,1:T(4,128)S(1)}, f32[4,20,20,2]{2,0,3,1:T(4,128)S(1)}, u32[]{:S(2)}, u32[]{:S(2)}) collective-permute-start(f32[4,20,20,2]{2,0,3,1:T(4,128)S(1)} %copy.314), channel_id=1, source_target_pairs={{0,1},{1,2},{2,3},{4,5},{5,6},{6,7},{8,9},{9,10},{10,11},{12,13},{... | collective-permute-start | bytes 38408 | tf_op jit(solution)/shard_map/ppermute | solution.py:21
  31.9 0.8 copy-start.7
  31.9 3.7 %copy-start = (f32[20,20,132]{2,1,0:T(8,128)}, f32[20,20,132]{2,1,0:T(8,128)S(1)}, u32[]{:S(2)}) copy-start(f32[20,20,132]{2,1,0:T(8,128)S(1)} %get-tuple-element.12) | copy-start | bytes 633604
  35.6 1.6 copy-start.9
  37.2 0.8 copy-start.11
  37.2 1.1 copy-start.6
  92.1 2.7 %collective-permute-start.7 = (f32[3,1,4,32]{3,2,1,0:T(4,128)S(1)}, f32[3,1,4,32]{3,2,1,0:T(4,128)S(1)}, u32[]{:S(2)}, u32[]{:S(2)}) collective-permute-start(f32[3,1,4,32]{3,2,1,0:T(4,128)S(1)} %multiply_divide_fusion.1), channel_id=1, source_target_pairs={{0,16},{1,17},{2,18},{3,19},{4,20},{5,21},{6,22},{7,23},{8,24},{9,... | collective-permute-start | bytes 4616 | tf_op jit(solution)/shard_map/ppermute | solution.py:21
  93.4 3.1 %collective-permute-start.6 = (f32[3,1,4,32]{3,2,1,0:T(4,128)S(1)}, f32[3,1,4,32]{3,2,1,0:T(4,128)S(1)}, u32[]{:S(2)}, u32[]{:S(2)}) collective-permute-start(f32[3,1,4,32]{3,2,1,0:T(4,128)S(1)} %multiply_divide_fusion.1), channel_id=1, source_target_pairs={{16,0},{17,1},{18,2},{19,3},{20,4},{21,5},{22,6},{23,7},{24,8},{25... | collective-permute-start | bytes 4616 | tf_op jit(solution)/shard_map/ppermute | solution.py:24
  96.8 3.4 %collective-permute-start.9 = (f32[3,1,4,32]{3,2,1,0:T(4,128)S(1)}, f32[3,1,4,32]{3,2,1,0:T(4,128)S(1)}, u32[]{:S(2)}, u32[]{:S(2)}) collective-permute-start(f32[3,1,4,32]{3,2,1,0:T(4,128)S(1)} %divide_add_fusion.5), channel_id=1, source_target_pairs={{0,16},{1,17},{2,18},{3,19},{4,20},{5,21},{6,22},{7,23},{8,24},{9,... | collective-permute-start | bytes 4616 | tf_op jit(solution)/shard_map/ppermute | solution.py:21
  98.9 3.1 %collective-permute-start.8 = (f32[3,1,4,32]{3,2,1,0:T(4,128)S(1)}, f32[3,1,4,32]{3,2,1,0:T(4,128)S(1)}, u32[]{:S(2)}, u32[]{:S(2)}) collective-permute-start(f32[3,1,4,32]{3,2,1,0:T(4,128)S(1)} %divide_add_fusion.5), channel_id=1, source_target_pairs={{16,0},{17,1},{18,2},{19,3},{20,4},{21,5},{22,6},{23,7},{24,8},{25... | collective-permute-start | bytes 4616 | tf_op jit(solution)/shard_map/ppermute | solution.py:24
  102.3 3.4 %collective-permute-start.11 = (f32[3,1,4,32]{3,2,1,0:T(4,128)S(1)}, f32[3,1,4,32]{3,2,1,0:T(4,128)S(1)}, u32[]{:S(2)}, u32[]{:S(2)}) collective-permute-start(f32[3,1,4,32]{3,2,1,0:T(4,128)S(1)} %divide_add_fusion.4), channel_id=1, source_target_pairs={{0,16},{1,17},{2,18},{3,19},{4,20},{5,21},{6,22},{7,23},{8,24},{9,... | collective-permute-start | bytes 4616 | tf_op jit(solution)/shard_map/ppermute | solution.py:21
  104.4 3.1 %collective-permute-start.10 = (f32[3,1,4,32]{3,2,1,0:T(4,128)S(1)}, f32[3,1,4,32]{3,2,1,0:T(4,128)S(1)}, u32[]{:S(2)}, u32[]{:S(2)}) collective-permute-start(f32[3,1,4,32]{3,2,1,0:T(4,128)S(1)} %divide_add_fusion.4), channel_id=1, source_target_pairs={{16,0},{17,1},{18,2},{19,3},{20,4},{21,5},{22,6},{23,7},{24,8},{25... | collective-permute-start | bytes 4616 | tf_op jit(solution)/shard_map/ppermute | solution.py:24
  107.8 3.6 %collective-permute-start.13 = (f32[3,1,4,32]{3,2,1,0:T(4,128)S(1)}, f32[3,1,4,32]{3,2,1,0:T(4,128)S(1)}, u32[]{:S(2)}, u32[]{:S(2)}) collective-permute-start(f32[3,1,4,32]{3,2,1,0:T(4,128)S(1)} %divide_add_fusion.3), channel_id=1, source_target_pairs={{0,16},{1,17},{2,18},{3,19},{4,20},{5,21},{6,22},{7,23},{8,24},{9,... | collective-permute-start | bytes 4616 | tf_op jit(solution)/shard_map/ppermute | solution.py:21
  109.9 3.1 %collective-permute-start.12 = (f32[3,1,4,32]{3,2,1,0:T(4,128)S(1)}, f32[3,1,4,32]{3,2,1,0:T(4,128)S(1)}, u32[]{:S(2)}, u32[]{:S(2)}) collective-permute-start(f32[3,1,4,32]{3,2,1,0:T(4,128)S(1)} %divide_add_fusion.3), channel_id=1, source_target_pairs={{16,0},{17,1},{18,2},{19,3},{20,4},{21,5},{22,6},{23,7},{24,8},{25... | collective-permute-start | bytes 4616 | tf_op jit(solution)/shard_map/ppermute | solution.py:24
  113.3 3.4 %collective-permute-start.15 = (f32[3,1,4,32]{3,2,1,0:T(4,128)S(1)}, f32[3,1,4,32]{3,2,1,0:T(4,128)S(1)}, u32[]{:S(2)}, u32[]{:S(2)}) collective-permute-start(f32[3,1,4,32]{3,2,1,0:T(4,128)S(1)} %divide_add_fusion.2), channel_id=1, source_target_pairs={{0,16},{1,17},{2,18},{3,19},{4,20},{5,21},{6,22},{7,23},{8,24},{9,... | collective-permute-start | bytes 4616 | tf_op jit(solution)/shard_map/ppermute | solution.py:21
  115.4 3.1 %collective-permute-start.14 = (f32[3,1,4,32]{3,2,1,0:T(4,128)S(1)}, f32[3,1,4,32]{3,2,1,0:T(4,128)S(1)}, u32[]{:S(2)}, u32[]{:S(2)}) collective-permute-start(f32[3,1,4,32]{3,2,1,0:T(4,128)S(1)} %divide_add_fusion.2), channel_id=1, source_target_pairs={{16,0},{17,1},{18,2},{19,3},{20,4},{21,5},{22,6},{23,7},{24,8},{25... | collective-permute-start | bytes 4616 | tf_op jit(solution)/shard_map/ppermute | solution.py:24
  118.8 3.4 %collective-permute-start.17 = (f32[3,1,4,32]{3,2,1,0:T(4,128)S(1)}, f32[3,1,4,32]{3,2,1,0:T(4,128)S(1)}, u32[]{:S(2)}, u32[]{:S(2)}) collective-permute-start(f32[3,1,4,32]{3,2,1,0:T(4,128)S(1)} %divide_add_fusion.1), channel_id=1, source_target_pairs={{0,16},{1,17},{2,18},{3,19},{4,20},{5,21},{6,22},{7,23},{8,24},{9,... | collective-permute-start | bytes 4616 | tf_op jit(solution)/shard_map/ppermute | solution.py:21
  120.9 3.1 %collective-permute-start.16 = (f32[3,1,4,32]{3,2,1,0:T(4,128)S(1)}, f32[3,1,4,32]{3,2,1,0:T(4,128)S(1)}, u32[]{:S(2)}, u32[]{:S(2)}) collective-permute-start(f32[3,1,4,32]{3,2,1,0:T(4,128)S(1)} %divide_add_fusion.1), channel_id=1, source_target_pairs={{16,0},{17,1},{18,2},{19,3},{20,4},{21,5},{22,6},{23,7},{24,8},{25... | collective-permute-start | bytes 4616 | tf_op jit(solution)/shard_map/ppermute | solution.py:24
  124.4 3.5 %collective-permute-start.19 = (f32[3,1,4,32]{3,2,1,0:T(4,128)S(1)}, f32[3,1,4,32]{3,2,1,0:T(4,128)S(1)}, u32[]{:S(2)}, u32[]{:S(2)}) collective-permute-start(f32[3,1,4,32]{3,2,1,0:T(4,128)S(1)} %divide_add_fusion), channel_id=1, source_target_pairs={{0,16},{1,17},{2,18},{3,19},{4,20},{5,21},{6,22},{7,23},{8,24},{9,... | collective-permute-start | bytes 4616 | tf_op jit(solution)/shard_map/ppermute | solution.py:21
  126.4 3.1 %collective-permute-start.18 = (f32[3,1,4,32]{3,2,1,0:T(4,128)S(1)}, f32[3,1,4,32]{3,2,1,0:T(4,128)S(1)}, u32[]{:S(2)}, u32[]{:S(2)}) collective-permute-start(f32[3,1,4,32]{3,2,1,0:T(4,128)S(1)} %divide_add_fusion), channel_id=1, source_target_pairs={{16,0},{17,1},{18,2},{19,3},{20,4},{21,5},{22,6},{23,7},{24,8},{25... | collective-permute-start | bytes 4616 | tf_op jit(solution)/shard_map/ppermute | solution.py:24
  130.3 13.6 %copy-start.4 = (f32[3,16,16,128]{3,2,1,0:T(8,128)}, f32[3,16,16,128]{3,2,1,0:T(8,128)S(1)}, u32[]{:S(2)}) copy-start(f32[3,16,16,128]{3,2,1,0:T(8,128)S(1)} %slice_add_fusion.52) | copy-start | bytes 1179652
  130.3 3.5 %collective-permute-start.20 = (f32[3,3,16,128]{3,2,1,0:T(8,128)S(1)}, f32[3,3,16,128]{3,2,1,0:T(8,128)S(1)}, u32[]{:S(2)}, u32[]{:S(2)}) collective-permute-start(f32[3,3,16,128]{3,2,1,0:T(8,128)S(1)} %get-tuple-element.26), channel_id=1, source_target_pairs={{0,16},{1,17},{2,18},{3,19},{4,20},{5,21},{6,22},{7,23},{8,24},{9,... | collective-permute-start | bytes 221192 | tf_op jit(solution)/shard_map/ppermute | solution.py:21
  132.4 3.2 %collective-permute-start.21 = (f32[3,3,16,128]{3,2,1,0:T(8,128)S(1)}, f32[3,3,16,128]{3,2,1,0:T(8,128)S(1)}, u32[]{:S(2)}, u32[]{:S(2)}) collective-permute-start(f32[3,3,16,128]{3,2,1,0:T(8,128)S(1)} %get-tuple-element.27), channel_id=1, source_target_pairs={{16,0},{17,1},{18,2},{19,3},{20,4},{21,5},{22,6},{23,7},{24,8},{25... | collective-permute-start | bytes 221192 | tf_op jit(solution)/shard_map/ppermute | solution.py:24
  135.6 8.3 %copy-start.16 = (f32[3,3,16,128]{3,2,1,0:T(8,128)}, f32[3,3,16,128]{3,2,1,0:T(8,128)S(1)}, u32[]{:S(2)}) copy-start(f32[3,3,16,128]{3,2,1,0:T(8,128)S(1)} %collective-permute-done.21) | copy-start | bytes 221188
  135.7 7.5 %collective-permute-start.23 = (f32[3,22,3,128]{3,1,2,0:T(8,128)S(1)}, f32[3,22,3,128]{3,1,2,0:T(8,128)S(1)}, u32[]{:S(2)}, u32[]{:S(2)}) collective-permute-start(f32[3,22,3,128]{3,1,2,0:T(8,128)S(1)} %copy.322), channel_id=1, source_target_pairs={{4,0},{8,4},{12,8},{5,1},{9,5},{13,9},{6,2},{10,6},{14,10},{7,3},{... | collective-permute-start | bytes 304136 | tf_op jit(solution)/shard_map/ppermute | solution.py:24
  137.0 6.9 %collective-permute-start.22 = (f32[3,22,3,128]{3,1,2,0:T(8,128)S(1)}, f32[3,22,3,128]{3,1,2,0:T(8,128)S(1)}, u32[]{:S(2)}, u32[]{:S(2)}) collective-permute-start(f32[3,22,3,128]{3,1,2,0:T(8,128)S(1)} %copy.321), channel_id=1, source_target_pairs={{0,4},{4,8},{8,12},{1,5},{5,9},{9,13},{2,6},{6,10},{10,14},{3,7},{... | collective-permute-start | bytes 304136 | tf_op jit(solution)/shard_map/ppermute | solution.py:21
  143.9 0.6 copy-start.14
  148.2 13.3 %copy-start.5 = (f32[3,16,16,128]{3,2,1,0:T(8,128)S(1)}, f32[3,16,16,128]{3,2,1,0:T(8,128)}, u32[]{:S(2)}) copy-start(f32[3,16,16,128]{3,2,1,0:T(8,128)} %copy-done.4) | copy-start | bytes 1179652
  149.3 9.9 %collective-permute-start.25 = (f32[3,22,22,3]{2,1,3,0:T(8,128)}, f32[3,22,22,3]{2,1,3,0:T(8,128)}, u32[]{:S(2)}, u32[]{:S(2)}) collective-permute-start(f32[3,22,22,3]{2,1,3,0:T(8,128)} %copy.326), channel_id=1, source_target_pairs={{1,0},{2,1},{3,2},{5,4},{6,5},{7,6},{9,8},{10,9},{11,10},{13,12},{... | collective-permute-start | bytes 52280 | tf_op jit(solution)/shard_map/ppermute | solution.py:24
  150.6 7.2 %collective-permute-start.24 = (f32[3,22,22,3]{2,1,3,0:T(8,128)}, f32[3,22,22,3]{2,1,3,0:T(8,128)}, u32[]{:S(2)}, u32[]{:S(2)}) collective-permute-start(f32[3,22,22,3]{2,1,3,0:T(8,128)} %copy.325), channel_id=1, source_target_pairs={{0,1},{1,2},{2,3},{4,5},{5,6},{6,7},{8,9},{9,10},{10,11},{12,13},{... | collective-permute-start | bytes 52280 | tf_op jit(solution)/shard_map/ppermute | solution.py:21
  166.9 1.4 copy-start.8
  166.9 1.4 copy-start.13
  168.3 1.0 copy-start.1
  172.5 1.4 copy-start.10
  172.5 1.4 copy-start.12
  175.8 1.4 copy-start.3
where the time goes:
time: 222 us; the launch traced here: 221 us
  blocking collectives  84.6 us (38%)
  starting transfers between devices  54.4 us (25%)
  other arithmetic  39.3 us (18%)
  waiting for transfers between devices  21.9 us (10%)
  local copies, waits for them, and re-layouts  18 us (8%)
  between operations  2.92 us (1%)
    all_gather x1, blocking collectives, coarse_correction(): lax.all_gather(local_sums[None], ('gy', 'gz'), axis=0, tiled=True)  43.3 us
    psum x1, blocking collectives, on_device(): residual_sum = lax.psum(jnp.sum(residual * residual), ('gx', 'gy', 'gz'))  41.3 us
    ppermute x13, starting transfers between devices, padded_2(): lax.ppermute(lax.slice_in_dim(block, block.shape[dim] - width, None, axis...  37.4 us
    ppermute x13, waiting for transfers between devices, padded_2(): lax.ppermute(lax.slice_in_dim(block, 0, width, axis=dim), axis, backward)  17.8 us
    ppermute x13, starting transfers between devices, padded_2(): lax.ppermute(lax.slice_in_dim(block, 0, width, axis=dim), axis, backward)  17 us
    another operation x11, other arithmetic, stencil(): return jnp.stack(images)  12 us
    add x24, other arithmetic, stencil(): coefficient * (6.0 * centre - beside_all + COUPLING * (axial_part - 0.25...  6.31 us
    concatenate x11, other arithmetic, padded_2(): block = jnp.concatenate([low, block, high], axis=dim)  5.4 us
  transfers between devices with their start and end apart: 26, of which 15 were waited for; matrix products, arithmetic and copies ran while one was open for 2% of the time, Pallas kernels for 0%

commit v1 on v0

v1 whole, which is shorter than its diff:
```python
import functools

import jax
import jax.numpy as jnp
from jax import lax
from jax.experimental import pallas as pl
from jax.experimental.pallas import tpu as pltpu
from jax.sharding import PartitionSpec as P

BLOCK = 16
COARSE = 8
FLOOR_STIFFNESS = 0.05
MASS_TERM = 0.001
COUPLING = 2.5
RELAXATION = 0.6
DIAGONAL = 6.0 + 2.0 * COUPLING
OWN = 1.0 + COUPLING
CROSS = 0.25 * COUPLING
AXES = ("gx", "gy", "gz")
HALO = 4
LANES = 128
MESH = pl.DeviceIdType.MESH
EXACT = lax.Precision.HIGHEST


def messages():
    out = []
    for dx in (-1, 1):
        for part in range(HALO):
            out.append(("x", dx, 0, 0, part))
    for part in range(2):
        for dy in (-1, 1):
            out.append(("y", 0, dy, 0, part))
        for dx in (-1, 1):
            for dy in (-1, 1):
                out.append(("xy", dx, dy, 0, part))
        if part == 0:
            for dz in (-1, 1):
                for dx in (-1, 0, 1):
                    for dy in (-1, 0, 1):
                        out.append(("z" if dx == 0 else "xz", dx, dy, dz, 0))
    return out


MESSAGES = messages()


def kernel(
    counts,
    extent,
    load_ref,
    damage_ref,
    out_ref,
    norms_ref,
    base,
    inverse,
    field_a,
    field_b,
    harm,
    y_send,
    y_recv,
    xy_send,
    xy_recv,
    z_send,
    z_recv,
    xz_send,
    xz_recv,
    coarse_send,
    coarse_recv,
    coarse_w,
    spread_w,
    norm_send,
    norm_recv,
    local_sem,
    send_sem,
    recv_sem,
    coarse_send_sem,
    coarse_recv_sem,
    norm_send_sem,
    norm_recv_sem,
):
    count_x, count_y, count_z = counts
    ex, ey, ez = extent
    cz = ez // BLOCK
    total = count_x * count_y * count_z
    wide_x = ex + 2 * HALO
    ypad = 8
    rows = ey + 2 * ypad
    wide_y = ey + 2 * HALO
    first_y = ypad - HALO
    me = tuple(lax.axis_index(axis) for axis in AXES)
    my_id = (me[0] * count_y + me[1]) * count_z + me[2]

    def place(index):
        return (
            index // (count_y * count_z),
            lax.rem(index // count_z, count_y),
            lax.rem(index, count_z),
        )

    load_copies = []
    for x in range(ex):
        target = pl.ds((HALO + x) * rows + ypad, ey)
        load_copies.append(
            pltpu.make_async_copy(load_ref.at[:, x], base.at[0, 0:3, target], local_sem.at[x])
        )
    harm_copy = pltpu.make_async_copy(damage_ref, harm, local_sem.at[ex])
    harm_copy.start()
    for copy in load_copies:
        copy.start()

    barrier = pltpu.get_barrier_semaphore()

    def greet(step, carry):
        pl.semaphore_signal(
            barrier,
            inc=1,
            device_id=place(lax.rem(my_id + step, total)),
            device_id_type=MESH,
        )
        return carry

    lax.fori_loop(1, total, greet, 0)

    harm_copy.wait()
    for x in range(ex):
        level = 1.0 - harm[x].astype(jnp.float32) / 15.0
        base[0, 3, pl.ds((HALO + x) * rows + ypad, ey)] = (
            level * level * (1.0 - FLOOR_STIFFNESS) + FLOOR_STIFFNESS
        )
    for copy in load_copies:
        copy.wait()

    lane = lax.broadcasted_iota(jnp.int32, (ey, LANES), 1)
    for side in range(2):
        for part in range(2):
            for layer in range(2):
                y = 2 * part + layer if side == 0 else ey - 2 - 2 * part + layer
                for f in range(4):
                    start = HALO * rows + ypad + y
                    for half in range(ex // 8):
                        y_send[side, part, f, layer, pl.ds(8 * half, 8)] = base[
                            0, f, pl.ds(start + 8 * half * rows, 8, stride=rows)
                        ]
                    for xs in range(2):
                        x0 = 0 if xs == 0 else ex - HALO
                        xy_send[xs, side, part, f, layer] = base[
                            0, f, pl.ds(start + x0 * rows, HALO, stride=rows)
                        ]
    for f in range(4):
        packed = None
        for k in range(ex):
            row = base[0, f, pl.ds((HALO + k) * rows + ypad, ey)]
            moved = pltpu.roll(row, (8 * k + HALO) % LANES, 1)
            packed = moved if packed is None else jnp.where(lane // 8 == k, moved, packed)
        z_send[f] = packed
    for xs in range(2):
        packed = None
        for f in range(4):
            for j in range(HALO):
                x = j if xs == 0 else ex - HALO + j
                k = f * HALO + j
                row = base[0, f, pl.ds((HALO + x) * rows + ypad, ey)]
                moved = pltpu.roll(row, (8 * k + HALO) % LANES, 1)
                packed = moved if packed is None else jnp.where(lane // 8 == k, moved, packed)
        xz_send[xs] = packed

    pl.semaphore_wait(barrier, total - 1)

    def exists(dx, dy, dz):
        ok = None
        for axis, step in enumerate((dx, dy, dz)):
            if step == 0:
                continue
            here = me[axis] + step
            good = (here >= 0) & (here < counts[axis])
            ok = good if ok is None else ok & good
        return ok

    def describe(number):
        kind, dx, dy, dz, part = MESSAGES[number]
        target = (me[0] + dx, me[1] + dy, me[2] + dz)
        xs, ys, zs = (dx + 1) // 2, (dy + 1) // 2, (dz + 1) // 2
        if kind == "x":
            src_x = HALO + part if dx < 0 else ex + part
            dst_x = HALO + ex + part if dx < 0 else part
            src = base.at[0, :, pl.ds(src_x * rows + ypad, ey)]
            dst = base.at[0, :, pl.ds(dst_x * rows + ypad, ey)]
        elif kind == "y":
            src, dst = y_send.at[ys, part], y_recv.at[1 - ys, part]
        elif kind == "xy":
            src, dst = xy_send.at[xs, ys, part], xy_recv.at[1 - xs, 1 - ys, part]
        else:
            if dy == 0:
                src_y, dst_y, size = 0, ypad, ey
            elif dy < 0:
                src_y, dst_y, size = 0, ypad + ey, ypad
            else:
                src_y, dst_y, size = ey - ypad, 0, ypad
            if kind == "z":
                src = z_send.at[:, pl.ds(src_y, size)]
                dst = z_recv.at[1 - zs, :, pl.ds(dst_y, size)]
            else:
                src = xz_send.at[xs, pl.ds(src_y, size)]
                dst = xz_recv.at[1 - xs, 1 - zs, pl.ds(dst_y, size)]
        copy = pltpu.make_async_remote_copy(
            src_ref=src,
            dst_ref=dst,
            send_sem=send_sem.at[number],
            recv_sem=recv_sem.at[number],
            device_id=target,
            device_id_type=MESH,
        )
        return copy, exists(dx, dy, dz), exists(-dx, -dy, -dz)

    for number in range(len(MESSAGES)):
        copy, to_there, _ = describe(number)

        @pl.when(to_there)
        def _():
            copy.start()

    def wait_for(part, send):
        for number, message in enumerate(MESSAGES):
            far = message[0] in ("y", "xy") and message[4] == 1
            if send and (message[0] == "x") != (part == 0):
                continue
            if not send and far != (part == 1):
                continue
            copy, to_there, from_there = describe(number)

            @pl.when(to_there if send else from_there)
            def _():
                if send:
                    copy.wait_send()
                else:
                    copy.wait_recv()

    def unpack_y(part):
        for side in range(2):
            for layer in range(2):
                y = (
                    ypad - 2 - 2 * part + layer
                    if side == 0
                    else ypad + ey + 2 * part + layer
                )
                for f in range(4):
                    for half in range(ex // 8):
                        base[
                            0, f, pl.ds((HALO + 8 * half) * rows + y, 8, stride=rows)
                        ] = y_recv[side, part, f, layer, pl.ds(8 * half, 8)]
                    for xs in range(2):
                        x0 = 0 if xs == 0 else HALO + ex
                        base[0, f, pl.ds(x0 * rows + y, HALO, stride=rows)] = xy_recv[
                            xs, side, part, f, layer
                        ]

    def unpack_z():
        lane_rows = lax.broadcasted_iota(jnp.int32, (rows, LANES), 1)
        lower = lax.rem(lane_rows, 8) < HALO
        for f in range(4):
            merged = jnp.where(lower, z_recv[0, f], z_recv[1, f])
            for k in range(ex):
                base[1, f, pl.ds((HALO + k) * rows, rows)] = pltpu.roll(
                    merged, (2 * LANES - 8 * k - HALO) % LANES, 1
                )
        for xs in range(2):
            merged = jnp.where(lower, xz_recv[xs, 0], xz_recv[xs, 1])
            for f in range(4):
                for j in range(HALO):
                    k = f * HALO + j
                    x = j if xs == 0 else HALO + ex + j
                    base[1, f, pl.ds(x * rows, rows)] = pltpu.roll(
                        merged, (2 * LANES - 8 * k - HALO) % LANES, 1
                    )

    lane = lax.broadcasted_iota(jnp.int32, (wide_y, LANES), 1)
    row_y = lax.broadcasted_iota(jnp.int32, (wide_y, LANES), 0)
    at_y = me[1] * ey + row_y - HALO
    good_y = (at_y >= 0) & (at_y < ey * count_y)
    good_halo = (
        good_y
        & ((me[2] > 0) | (lane < LANES // 2))
        & ((me[2] < count_z - 1) | (lane >= LANES // 2))
    )
    goods = (good_y, good_halo)

    def at(x, dy=0):
        return pl.ds(x * rows + first_y + dy, wide_y)

    def prepare(x, carry):
        at_x = me[0] * ex + x - HALO
        good_x = (at_x >= 0) & (at_x < ex * count_x)
        for t in range(2):
            good = goods[t] & good_x
            g = jnp.where(good, base[t, 3, at(x)], 1.0)
            base[t, 3, at(x)] = g
            inv = jnp.where(good, RELAXATION / (g * DIAGONAL + MASS_TERM), 0.0)
            inverse[t, at(x)] = inv
            for c in range(3):
                load = jnp.where(good, base[t, c, at(x)], 0.0)
                base[t, c, at(x)] = load
                field_a[t, c, at(x)] = load * inv
        return carry

    first_lane = lane == 0
    last_lane = lane == LANES - 1

    def image(field, x):
        parts = [[None] * 3, [None] * 3]
        ups = [[None] * 3, [None] * 3]
        downs = [[None] * 3, [None] * 3]
        for t in range(2):

            def load(c, ox, oy):
                return field[t, c, at(x + ox, oy)]

            centre = [load(c, 0, 0) for c in range(3)]
            x_up = [load(c, 1, 0) for c in range(3)]
            x_down = [load(c, -1, 0) for c in range(3)]
            y_up = [load(c, 0, 1) for c in range(3)]
            y_down = [load(c, 0, -1) for c in range(3)]

            def corners(c):
                return (load(c, 1, 1) - load(c, 1, -1)) - (load(c, -1, 1) - load(c, -1, -1))

            sum_x = [x_up[c] + x_down[c] for c in range(3)]
            sum_y = [y_up[c] + y_down[c] for c in range(3)]
            parts[t][0] = DIAGONAL * centre[0] - OWN * sum_x[0] - sum_y[0] - CROSS * corners(1)
            parts[t][1] = DIAGONAL * centre[1] - sum_x[1] - OWN * sum_y[1] - CROSS * corners(0)
            parts[t][2] = DIAGONAL * centre[2] - sum_x[2] - sum_y[2]
            tilt_x = CROSS * (x_up[2] - x_down[2])
            tilt_y = CROSS * (y_up[2] - y_down[2])
            tilt_z = CROSS * ((x_up[0] - x_down[0]) + (y_up[1] - y_down[1]))
            own_z = OWN * centre[2]
            ups[t] = [centre[0] + tilt_x, centre[1] + tilt_y, own_z + tilt_z]
            downs[t] = [centre[0] - tilt_x, centre[1] - tilt_y, own_z - tilt_z]
        out = [[None] * 3, [None] * 3]
        for c in range(3):
            up = [pltpu.roll(ups[t][c], LANES - 1, 1) for t in range(2)]
            down = [pltpu.roll(downs[t][c], 1, 1) for t in range(2)]
            for t in range(2):
                beside = jnp.where(last_lane, up[1 - t], up[t]) + jnp.where(
                    first_lane, down[1 - t], down[t]
                )
                out[t][c] = parts[t][c] - beside
        return out

    def residual(field, x, tiles):
        images = image(field, x)
        out = []
        for t in tiles:
            g = base[t, 3, at(x)]
            out.append(
                [
                    base[t, c, at(x)] - (g * images[t][c] + MASS_TERM * field[t, c, at(x)])
                    for c in range(3)
                ]
            )
        return out

    def sweep(source, target, low, high):
        def one(x, carry):
            left = residual(source, x, (0, 1))
            for t in range(2):
                inv = inverse[t, at(x)]
                for c in range(3):
                    target[t, c, at(x)] = source[t, c, at(x)] + inv * left[t][c]
            return carry

        lax.fori_loop(low, high, one, 0)

    inner_y = (row_y >= HALO) & (row_y < HALO + ey)

    def fold(value):
        return jnp.sum(value.reshape(wide_y // 8, 8, LANES), axis=0)

    zero = jnp.zeros((8, LANES), jnp.float32)

    wait_for(0, False)
    wait_for(0, True)
    unpack_y(0)
    unpack_z()
    lax.fori_loop(2, wide_x - 2, prepare, 0)
    sweep(field_a, field_b, 3, wide_x - 3)

    def restrict(x, carry):
        left = residual(field_b, x, (0,))[0]
        sums = [
            carry[c] + fold(jnp.where(inner_y, left[c], 0.0)) for c in range(3)
        ]
        sums.append(carry[3] + fold(jnp.where(inner_y, base[0, 3, at(x)], 0.0)))
        return tuple(sums)

    sums = lax.fori_loop(HALO, HALO + ex, restrict, (zero,) * 4)
    stacked = jnp.concatenate([jnp.sum(s, axis=0, keepdims=True) for s in sums] + [zero[:4]], axis=0)
    source_lane = lax.broadcasted_iota(jnp.int32, (LANES, LANES), 0)
    target_lane = lax.broadcasted_iota(jnp.int32, (LANES, LANES), 1)
    gather = (source_lane // BLOCK == lax.rem(target_lane, cz)).astype(jnp.float32)
    grouped = jnp.dot(stacked, gather, precision=EXACT, preferred_element_type=jnp.float32)
    coarse_send[...] = grouped[:4]

    reach = -(-COARSE // cz)
    window = 2 * reach + 1

    def peers(act):
        for dz in range(-reach, reach + 1):
            z = me[2] + dz

            @pl.when((z >= 0) & (z < count_z))
            def _():
                def one(step, carry):
                    if dz == 0:
                        step = step + 1
                    index = lax.rem(me[0] * count_y + me[1] + step, count_x * count_y)
                    act(index // count_y, lax.rem(index, count_y), z, dz)
                    return carry

                lax.fori_loop(0, count_x * count_y - (1 if dz == 0 else 0), one, 0)

    def coarse_copy(x, y, z, dz):
        return pltpu.make_async_remote_copy(
            src_ref=coarse_send,
            dst_ref=coarse_recv.at[reach - dz, me[0], me[1]],
            send_sem=coarse_send_sem.at[reach + dz, x, y],
            recv_sem=coarse_recv_sem.at[reach - dz, me[0], me[1]],
            device_id=(x, y, z),
            device_id_type=MESH,
        )

    def coarse_wait(x, y, z, dz):
        pltpu.make_async_remote_copy(
            src_ref=coarse_send,
            dst_ref=coarse_recv.at[reach + dz, x, y],
            send_sem=coarse_send_sem.at[reach + dz, x, y],
            recv_sem=coarse_recv_sem.at[reach + dz, x, y],
            device_id=(x, y, z),
            device_id_type=MESH,
        ).wait()

    peers(lambda x, y, z, dz: coarse_copy(x, y, z, dz).start())
    coarse_recv[reach, me[0], me[1]] = grouped[:4]

    wait_for(1, False)
    unpack_y(1)
    lax.fori_loop(0, wide_x, prepare, 0)
    sweep(field_a, field_b, 1, wide_x - 1)
    wait_for(1, True)
    peers(coarse_wait)

    coarse_rows = -(-(count_y + 1) // 8) * 8
    lane_c = lax.broadcasted_iota(jnp.int32, (coarse_rows, LANES), 1)
    row_c = lax.broadcasted_iota(jnp.int32, (coarse_rows, LANES), 0)
    at_z = me[2] * cz - reach * cz + lane_c
    valid = (
        (row_c < count_y) & (at_z >= 0) & (at_z < cz * count_z) & (lane_c < window * cz)
    )
    slab = [[None] * 4 for _ in range(count_x)]
    for x in range(count_x):
        for c in range(4):
            value = None
            for w in range(window):
                column = jnp.concatenate(
                    [coarse_recv[w, x, y, c : c + 1] for y in range(count_y)]
                    + [jnp.zeros((coarse_rows - count_y, LANES), jnp.float32)],
                    axis=0,
                )
                value = column if value is None else jnp.where(lane_c // cz == w, column, value)
            slab[x][c] = jnp.where(valid, value, 0.0)
    mass = BLOCK**3 * MASS_TERM
    factor = [slab[x][3] * (BLOCK**2 / BLOCK**3) for x in range(count_x)]
    relax = [
        jnp.where(valid, RELAXATION / (factor[x] * DIAGONAL + mass), 0.0) for x in range(count_x)
    ]
    nothing = jnp.zeros((coarse_rows, LANES), jnp.float32)
    w = [[slab[x][c] * relax[x] for c in range(3)] for x in range(count_x)]

    def y_shift(value, step):
        return pltpu.roll(value, step % coarse_rows, 0)

    def z_shift(value, step):
        return pltpu.roll(value, step % LANES, 1)

    for repeat in range(COARSE - 1):
        fresh = []
        for x in range(count_x):
            here = w[x]
            above = w[x + 1] if x + 1 < count_x else [nothing] * 3
            below = w[x - 1] if x > 0 else [nothing] * 3
            sum_x = [above[c] + below[c] for c in range(3)]
            diff_x = [above[c] - below[c] for c in range(3)]
            y_up = [y_shift(here[c], -1) for c in range(3)]
            y_down = [y_shift(here[c], 1) for c in range(3)]
            sum_y = [y_up[c] + y_down[c] for c in range(3)]
            diff_y = [y_up[c] - y_down[c] for c in range(3)]
            corner_x = y_shift(diff_x[1], -1) - y_shift(diff_x[1], 1)
            corner_y = y_shift(diff_x[0], -1) - y_shift(diff_x[0], 1)
            tilt = [CROSS * diff_x[2], CROSS * diff_y[2], CROSS * (diff_x[0] + diff_y[1])]
            own = [here[0], here[1], OWN * here[2]]
            beside = [z_shift(own[c] + tilt[c], -1) + z_shift(own[c] - tilt[c], 1) for c in range(3)]
            flat = [
                DIAGONAL * here[0] - OWN * sum_x[0] - sum_y[0] - CROSS * corner_x - beside[0],
                DIAGONAL * here[1] - sum_x[1] - OWN * sum_y[1] - CROSS * corner_y - beside[1],
                DIAGONAL * here[2] - sum_x[2] - sum_y[2] - beside[2],
            ]
            fresh.append(
                [
                    here[c] + relax[x] * (slab[x][c] - (factor[x] * flat[c] + mass * here[c]))
                    for c in range(3)
                ]
            )
        w = fresh

    for x in range(count_x + 2):
        for c in range(3):
            inside = 1 <= x <= count_x
            coarse_w[x, c, pl.ds(0, 8)] = jnp.zeros((8, LANES), jnp.float32)
            coarse_w[x, c, pl.ds(8, coarse_rows)] = w[x - 1][c] if inside else nothing
    widen_core = (source_lane == reach * cz + target_lane // BLOCK).astype(jnp.float32)
    widen_halo = (
        source_lane == jnp.where(target_lane < LANES // 2, (reach + 1) * cz, reach * cz - 1)
    ).astype(jnp.float32)
    for xc in range(3):
        for c in range(3):
            cells = [coarse_w[me[0] + xc, c, pl.ds(7 + me[1] + k, 1)] for k in range(3)]
            stacked = jnp.concatenate(cells + [zero[:5]], axis=0)
            for t, matrix in enumerate((widen_core, widen_halo)):
                wide = jnp.dot(stacked, matrix, precision=EXACT, preferred_element_type=jnp.float32)
                low = jnp.broadcast_to(wide[0:1], (wide_y, LANES))
                mid = jnp.broadcast_to(wide[1:2], (wide_y, LANES))
                top = jnp.broadcast_to(wide[2:3], (wide_y, LANES))
                spread_w[t, c, xc] = jnp.where(
                    row_y < HALO, low, jnp.where(row_y < HALO + ey, mid, top)
                )

    def correct(x, carry):
        cell = (x + ex - HALO) // ex
        for t in range(2):
            for c in range(3):
                field_b[t, c, at(x)] = field_b[t, c, at(x)] + spread_w[t, c, cell]
        return carry

    lax.fori_loop(1, wide_x - 1, correct, 0)
    sweep(field_b, field_a, 2, wide_x - 2)
    sweep(field_a, field_b, 3, wide_x - 3)
    out_copies = []
    for x in range(ex):
        copy = pltpu.make_async_copy(
            field_b.at[0, :, pl.ds((HALO + x) * rows + ypad, ey)],
            out_ref.at[:, x],
            local_sem.at[x],
        )
        copy.start()
        out_copies.append(copy)

    def squares(x, carry):
        left = residual(field_b, x, (0,))[0]
        both = []
        square = sum(value * value for value in left)
        loads = [base[0, c, at(x)] for c in range(3)]
        load_square = sum(value * value for value in loads)
        both.append(carry[0] + fold(jnp.where(inner_y, load_square, 0.0)))
        both.append(carry[1] + fold(jnp.where(inner_y, square, 0.0)))
        return tuple(both)

    load_sum, left_sum = lax.fori_loop(HALO, HALO + ex, squares, (zero, zero))
    load_total = jnp.sum(jnp.sum(load_sum, axis=0, keepdims=True), axis=1, keepdims=True)
    left_total = jnp.sum(jnp.sum(left_sum, axis=0, keepdims=True), axis=1, keepdims=True)
    first = lax.broadcasted_iota(jnp.int32, (1, LANES), 1) == 0
    mine = jnp.where(first, load_total, left_total)
    norm_send[...] = mine

    def norm_copy(step):
        return pltpu.make_async_remote_copy(
            src_ref=norm_send,
            dst_ref=norm_recv.at[step - 1],
            send_sem=norm_send_sem.at[step - 1],
            recv_sem=norm_recv_sem.at[step - 1],
            device_id=place(lax.rem(my_id + step, total)),
            device_id_type=MESH,
        )

    def norm_start(step, carry):
        norm_copy(step).start()
        return carry

    def norm_wait(step, carry):
        norm_copy(step).wait()
        return carry

    lax.fori_loop(1, total, norm_start, 0)
    norm_recv[total - 1] = mine
    for copy in out_copies:
        copy.wait()
    lax.fori_loop(1, total, norm_wait, 0)

    def add(device, carry):
        slot = lax.rem(my_id - device + total - 1, total)
        return carry + norm_recv[lax.rem(slot + total, total)]

    summed = lax.fori_loop(0, total, add, jnp.zeros((1, LANES), jnp.float32))
    nodes = 3 * ex * ey * ez * total
    norms_ref[...] = jnp.sqrt(summed / nodes)


def on_device(counts, right_side, damage):
    _, ex, ey, ez = right_side.shape
    cz = ez // BLOCK
    wide_x = ex + 2 * HALO
    rows = ey + 16
    flat = wide_x * rows
    wide_y = ey + 2 * HALO
    total = counts[0] * counts[1] * counts[2]
    window = 2 * (-(-COARSE // cz)) + 1
    coarse_rows = -(-(counts[1] + 1) // 8) * 8
    f32 = jnp.float32
    vmem = pltpu.VMEM
    dma = pltpu.SemaphoreType.DMA
    displacement, norms = pl.pallas_call(
        functools.partial(kernel, counts, (ex, ey, ez)),
        out_shape=(
            jax.ShapeDtypeStruct(right_side.shape, f32),
            jax.ShapeDtypeStruct((1, LANES), f32),
        ),
        in_specs=[pl.BlockSpec(memory_space=pl.ANY)] * 2,
        out_specs=(
            pl.BlockSpec(memory_space=pl.ANY),
            pl.BlockSpec(memory_space=pltpu.VMEM),
        ),
        scratch_shapes=[
            vmem((2, 4, flat, LANES), f32),
            vmem((2, flat, LANES), f32),
            vmem((2, 3, flat, LANES), f32),
            vmem((2, 3, flat, LANES), f32),
            vmem((ex, ey, LANES), jnp.int32),
            vmem((2, 2, 4, 2, ex, LANES), f32),
            vmem((2, 2, 4, 2, ex, LANES), f32),
            vmem((2, 2, 2, 4, 2, HALO, LANES), f32),
            vmem((2, 2, 2, 4, 2, HALO, LANES), f32),
            vmem((4, ey, LANES), f32),
            vmem((2, 4, rows, LANES), f32),
            vmem((2, ey, LANES), f32),
            vmem((2, 2, rows, LANES), f32),
            vmem((4, LANES), f32),
            vmem((window, counts[0], counts[1], 4, LANES), f32),
            vmem((counts[0] + 2, 3, 8 + coarse_rows, LANES), f32),
            vmem((2, 3, 3, wide_y, LANES), f32),
            vmem((1, LANES), f32),
            vmem((total, 1, LANES), f32),
            dma((ex + 1,)),
            dma((len(MESSAGES),)),
            dma((len(MESSAGES),)),
            dma((window, counts[0], counts[1])),
            dma((window, counts[0], counts[1])),
            dma((total,)),
            dma((total,)),
        ],
        compiler_params=pltpu.CompilerParams(collective_id=0, has_side_effects=True),
    )(right_side, damage)
    return displacement, norms[0, :2]


def solution(mesh):
    counts = tuple(mesh.shape[axis] for axis in AXES)
    placed = (P(None, "gx", "gy", "gz"), P("gx", "gy", "gz"))
    return jax.shard_map(
        functools.partial(on_device, counts),
        mesh=mesh,
        in_specs=placed,
        out_specs=(P(None, "gx", "gy", "gz"), P()),
        check_vma=False,
    )
```

time: 222 us -> 42.4 us (0.19)
  blocking collectives: 84.6 us -> 0 us
  starting transfers between devices: 54.4 us -> 0 us
  other arithmetic: 39.3 us -> 0 us
  Pallas kernels: 0 us -> 38.7 us
  waiting for transfers between devices: 21.9 us -> 0 us
  local copies, waits for them, and re-layouts: 18 us -> 2.95 us
  between operations: 2.92 us -> 0.65 us
    ppermute x26 -> x0, starting transfers between devices: 54.4 us -> none  [the longest x13 37.4 us: padded_2(): lax.ppermute(lax.slice_in_dim(block, block.shape[dim] - width, None, axis...]
    all_gather x1 -> x0, blocking collectives: 43.3 us -> none  [coarse_correction(): lax.all_gather(local_sums[None], ('gy', 'gz'), axis=0, tiled=True)]
    psum x1 -> x0, blocking collectives: 41.3 us -> none  [on_device(): residual_sum = lax.psum(jnp.sum(residual * residual), ('gx', 'gy', 'gz'))]
    pallas_call x0 -> x1, Pallas kernels: none -> 38.7 us  [on_device(): pl.pallas_call(functools.partial(kernel, counts, (ex, ey, ez)), out_shape...]
    ppermute x26 -> x0, waiting for transfers between devices: 21.9 us -> none  [the longest x13 17.8 us: padded_2(): lax.ppermute(lax.slice_in_dim(block, 0, width, axis=dim), axis, backward)]
    another operation x12 -> x0, other arithmetic: 12.6 us -> none  [the longest x11 12 us: stencil(): return jnp.stack(images)]
    add x34 -> x0, other arithmetic: 8.2 us -> none  [the longest x24 6.31 us: stencil(): coefficient * (6.0 * centre - beside_all + COUPLING * (axial_part - 0.25...]
    slice x12 -> x0, local copies, waits for them, and re-layouts: 7.2 us -> none  [the longest x6 4.42 us: padded_2(): lax.slice_in_dim(block, block.shape[dim] - width, None, axis=dim)]
  transfers between devices with their start and end apart: 26 -> 0, of which waited for: 15 -> 0; matrix products, arithmetic and copies ran while one was open for 2% -> 0% of each run, Pallas kernels for 0% -> 0%
where the time goes in v1:
time: 42.4 us; the launch traced here: 42.3 us
  Pallas kernels  38.7 us (91%)
  local copies, waits for them, and re-layouts  2.95 us (7%)
  between operations  0.65 us (2%)
    pallas_call x1, Pallas kernels, on_device(): pl.pallas_call(functools.partial(kernel, counts, (ex, ey, ez)), out_shape...  38.7 us
    unnamed x3, local copies, waits for them, and re-layouts  2.44 us

profile of v1, /device:TPU:0, one launch (start us, length us, event | category | flops | bytes accessed | tf_op | source)
XLA Modules:
  0.0 42.3 jit_solution(18095466421081064)
XLA Ops:
  0.6 38.7 %shard_map.41 = (f32[3,16,16,128]{3,2,1,0:T(8,128)}, f32[1,128]{1,0:T(1,128)}) custom-call(f32[3,16,16,128]{3,2,1,0:T(8,128)} %load_ref.1, s32[16,16,128]{2,1,0:T(8,128)} %damage_ref.1), custom_call_target="tpu_custom_call" | custom-call | tf_op jit(solution)/shard_map/pallas_call | solution.py:619
  39.3 0.0 copy-start
  39.3 0.7 %copy-done = f32[1,128]{1,0:T(1,128)S(1)} copy-done((f32[1,128]{1,0:T(1,128)S(1)}, f32[1,128]{1,0:T(1,128)}, u32[]{:S(2)}) %copy-start) | copy-done | bytes 536
  40.0 0.5 %slice_bitcast_fusion = f32[2]{0:T(128)} fusion(f32[1,128]{1,0:T(1,128)S(1)} %copy-done), kind=kLoop, calls=%fused_computation | loop fusion | bytes 16 | tf_op jit(solution)/shard_map/squeeze | solution.py:660
  40.5 1.8 %copy.5 = f32[3,16,16,128]{3,2,1,0:T(8,128)} copy(f32[3,16,16,128]{3,2,1,0:T(8,128)} %get-tuple-element.8) | data formatting | bytes 786432
Async XLA Ops:
  39.3 0.7 %copy-start = (f32[1,128]{1,0:T(1,128)S(1)}, f32[1,128]{1,0:T(1,128)}, u32[]{:S(2)}) copy-start(f32[1,128]{1,0:T(1,128)} %get-tuple-element.5) | copy-start | bytes 1540

commit v2 on v1

--- a/solution.py
+++ b/solution.py
@@ -69,6 +69,7 @@
     coarse_recv,
     coarse_w,
     spread_w,
+    image_w,
     norm_send,
     norm_recv,
     local_sem,
@@ -78,6 +79,7 @@
     coarse_recv_sem,
     norm_send_sem,
     norm_recv_sem,
+    hello_sem,
 ):
     count_x, count_y, count_z = counts
     ex, ey, ez = extent
@@ -111,16 +113,29 @@
 
     barrier = pltpu.get_barrier_semaphore()
 
-    def greet(step, carry):
-        pl.semaphore_signal(
-            barrier,
-            inc=1,
-            device_id=place(lax.rem(my_id + step, total)),
-            device_id_type=MESH,
-        )
-        return carry
-
-    lax.fori_loop(1, total, greet, 0)
+    reach = -(-COARSE // cz)
+    window = 2 * reach + 1
+
+    def peers(act):
+        for dz in range(-reach, reach + 1):
+            z = me[2] + dz
+
+            @pl.when((z >= 0) & (z < count_z))
+            def _():
+                def one(step, carry):
+                    if dz == 0:
+                        step = step + 1
+                    index = lax.rem(me[0] * count_y + me[1] + step, count_x * count_y)
+                    act(index // count_y, lax.rem(index, count_y), z, dz)
+                    return carry
+
+                lax.fori_loop(0, count_x * count_y - (1 if dz == 0 else 0), one, 0)
+
+    def greet(x, y, z, dz):
+        pl.semaphore_signal(barrier, inc=1, device_id=(x, y, z), device_id_type=MESH)
+
+    peers(greet)
+    levels = jnp.minimum(me[2] + reach, count_z - 1) - jnp.maximum(me[2] - reach, 0) + 1
 
     harm_copy.wait()
     for x in range(ex):
@@ -165,7 +180,7 @@
                 packed = moved if packed is None else jnp.where(lane // 8 == k, moved, packed)
         xz_send[xs] = packed
 
-    pl.semaphore_wait(barrier, total - 1)
+    pl.semaphore_wait(barrier, levels * count_x * count_y - 1)
 
     def exists(dx, dy, dz):
         ok = None
@@ -220,6 +235,34 @@
         def _():
             copy.start()
 
+    rounds = []
+    radius = reach
+    while radius < count_z - 1:
+        rounds.append(radius)
+        radius *= 2
+
+    def hello(number):
+        for side, step in enumerate((-rounds[number], rounds[number])):
+
+            @pl.when(exists(0, 0, step))
+            def _():
+                pl.semaphore_signal(
+                    hello_sem.at[number, 1 - side],
+                    inc=1,
+                    device_id=(me[0], me[1], me[2] + step),
+                    device_id_type=MESH,
+                )
+
+    def hear(number):
+        for side, step in enumerate((-rounds[number], rounds[number])):
+
+            @pl.when(exists(0, 0, step))
+            def _():
+                pl.semaphore_wait(hello_sem.at[number, side], 1)
+
+    if rounds:
+        hello(0)
+
     def wait_for(part, send):
         for number, message in enumerate(MESSAGES):
             far = message[0] in ("y", "xy") and message[4] == 1
@@ -285,7 +328,9 @@
     )
     goods = (good_y, good_halo)
 
-    def at(x, dy=0):
+    def at(x, dy=0, own=False):
+        if own:
+            return pl.ds(x * rows + ypad + dy, ey)
         return pl.ds(x * rows + first_y + dy, wide_y)
 
     def prepare(x, carry):
@@ -303,17 +348,14 @@
                 field_a[t, c, at(x)] = load * inv
         return carry
 
-    first_lane = lane == 0
-    last_lane = lane == LANES - 1
-
-    def image(field, x):
+    def image(field, x, own=False):
         parts = [[None] * 3, [None] * 3]
         ups = [[None] * 3, [None] * 3]
         downs = [[None] * 3, [None] * 3]
         for t in range(2):
 
             def load(c, ox, oy):
-                return field[t, c, at(x + ox, oy)]
+                return field[t, c, at(x + ox, oy, own)]
 
             centre = [load(c, 0, 0) for c in range(3)]
             x_up = [load(c, 1, 0) for c in range(3)]
@@ -336,6 +378,9 @@
             ups[t] = [centre[0] + tilt_x, centre[1] + tilt_y, own_z + tilt_z]
             downs[t] = [centre[0] - tilt_x, centre[1] - tilt_y, own_z - tilt_z]
         out = [[None] * 3, [None] * 3]
+        lanes = lax.broadcasted_iota(jnp.int32, parts[0][0].shape, 1)
+        first_lane = lanes == 0
+        last_lane = lanes == LANES - 1
         for c in range(3):
             up = [pltpu.roll(ups[t][c], LANES - 1, 1) for t in range(2)]
             down = [pltpu.roll(downs[t][c], 1, 1) for t in range(2)]
@@ -346,14 +391,15 @@
                 out[t][c] = parts[t][c] - beside
         return out
 
-    def residual(field, x, tiles):
-        images = image(field, x)
+    def residual(field, x, tiles, own=False):
+        images = image(field, x, own)
         out = []
+        here = at(x, 0, own)
         for t in tiles:
-            g = base[t, 3, at(x)]
+            g = base[t, 3, here]
             out.append(
                 [
-                    base[t, c, at(x)] - (g * images[t][c] + MASS_TERM * field[t, c, at(x)])
+                    base[t, c, here] - (g * images[t][c] + MASS_TERM * field[t, c, here])
                     for c in range(3)
                 ]
             )
@@ -370,10 +416,8 @@
 
         lax.fori_loop(low, high, one, 0)
 
-    inner_y = (row_y >= HALO) & (row_y < HALO + ey)
-
     def fold(value):
-        return jnp.sum(value.reshape(wide_y // 8, 8, LANES), axis=0)
+        return jnp.sum(value.reshape(ey // 8, 8, LANES), axis=0)
 
     zero = jnp.zeros((8, LANES), jnp.float32)
 
@@ -385,11 +429,9 @@
     sweep(field_a, field_b, 3, wide_x - 3)
 
     def restrict(x, carry):
-        left = residual(field_b, x, (0,))[0]
-        sums = [
-            carry[c] + fold(jnp.where(inner_y, left[c], 0.0)) for c in range(3)
-        ]
-        sums.append(carry[3] + fold(jnp.where(inner_y, base[0, 3, at(x)], 0.0)))
+        left = residual(field_b, x, (0,), True)[0]
+        sums = [carry[c] + fold(left[c]) for c in range(3)]
+        sums.append(carry[3] + fold(base[0, 3, at(x, 0, True)]))
         return tuple(sums)
 
     sums = lax.fori_loop(HALO, HALO + ex, restrict, (zero,) * 4)
@@ -399,24 +441,6 @@
     gather = (source_lane // BLOCK == lax.rem(target_lane, cz)).astype(jnp.float32)
     grouped = jnp.dot(stacked, gather, precision=EXACT, preferred_element_type=jnp.float32)
     coarse_send[...] = grouped[:4]
-
-    reach = -(-COARSE // cz)
-    window = 2 * reach + 1
-
-    def peers(act):
-        for dz in range(-reach, reach + 1):
-            z = me[2] + dz
-
-            @pl.when((z >= 0) & (z < count_z))
-            def _():
-                def one(step, carry):
-                    if dz == 0:
-                        step = step + 1
-                    index = lax.rem(me[0] * count_y + me[1] + step, count_x * count_y)
-                    act(index // count_y, lax.rem(index, count_y), z, dz)
-                    return carry
-
-                lax.fori_loop(0, count_x * count_y - (1 if dz == 0 else 0), one, 0)
 
     def coarse_copy(x, y, z, dz):
         return pltpu.make_async_remote_copy(
@@ -445,7 +469,18 @@
     unpack_y(1)
     lax.fori_loop(0, wide_x, prepare, 0)
     sweep(field_a, field_b, 1, wide_x - 1)
+    sweep(field_b, field_a, 2, wide_x - 2)
+
+    def load_squares(x, carry):
+        loads = [base[0, c, at(x, 0, True)] for c in range(3)]
+        return carry + fold(sum(value * value for value in loads))
+
+    load_sum = lax.fori_loop(HALO, HALO + ex, load_squares, zero)
     wait_for(1, True)
+    for number in range(len(rounds)):
+        if number > 0:
+            hello(number)
+        hear(number)
     peers(coarse_wait)
 
     coarse_rows = -(-(count_y + 1) // 8) * 8
@@ -529,41 +564,47 @@
                 low = jnp.broadcast_to(wide[0:1], (wide_y, LANES))
                 mid = jnp.broadcast_to(wide[1:2], (wide_y, LANES))
                 top = jnp.broadcast_to(wide[2:3], (wide_y, LANES))
-                spread_w[t, c, xc] = jnp.where(
-                    row_y < HALO, low, jnp.where(row_y < HALO + ey, mid, top)
-                )
-
-    def correct(x, carry):
-        cell = (x + ex - HALO) // ex
+                wide = jnp.where(row_y < HALO, low, jnp.where(row_y < HALO + ey, mid, top))
+                for plane in range(3):
+                    spread_w[t, c, pl.ds((3 * xc + plane) * rows + first_y, wide_y)] = wide
+    for plane in range(1, 8):
+        images = image(spread_w, plane)
         for t in range(2):
             for c in range(3):
-                field_b[t, c, at(x)] = field_b[t, c, at(x)] + spread_w[t, c, cell]
+                image_w[t, c, at(plane)] = images[t][c]
+
+    def correct(x, carry):
+        kind = (
+            1
+            + (x >= HALO - 1).astype(jnp.int32)
+            + (x >= HALO).astype(jnp.int32)
+            + (x >= HALO + 1).astype(jnp.int32)
+            + (x >= HALO + ex - 1).astype(jnp.int32)
+            + (x >= HALO + ex).astype(jnp.int32)
+            + (x >= HALO + ex + 1).astype(jnp.int32)
+        )
+        for t in range(2):
+            inv = inverse[t, at(x)]
+            g = base[t, 3, at(x)]
+            for c in range(3):
+                added = spread_w[t, c, at(kind)]
+                field_a[t, c, at(x)] = (
+                    field_a[t, c, at(x)]
+                    + added
+                    - inv * (g * image_w[t, c, at(kind)] + MASS_TERM * added)
+                )
         return carry
 
-    lax.fori_loop(1, wide_x - 1, correct, 0)
-    sweep(field_b, field_a, 2, wide_x - 2)
+    lax.fori_loop(2, wide_x - 2, correct, 0)
     sweep(field_a, field_b, 3, wide_x - 3)
-    out_copies = []
-    for x in range(ex):
-        copy = pltpu.make_async_copy(
-            field_b.at[0, :, pl.ds((HALO + x) * rows + ypad, ey)],
-            out_ref.at[:, x],
-            local_sem.at[x],
-        )
-        copy.start()
-        out_copies.append(copy)
 
     def squares(x, carry):
-        left = residual(field_b, x, (0,))[0]
-        both = []
-        square = sum(value * value for value in left)
-        loads = [base[0, c, at(x)] for c in range(3)]
-        load_square = sum(value * value for value in loads)
-        both.append(carry[0] + fold(jnp.where(inner_y, load_square, 0.0)))
-        both.append(carry[1] + fold(jnp.where(inner_y, square, 0.0)))
-        return tuple(both)
-
-    load_sum, left_sum = lax.fori_loop(HALO, HALO + ex, squares, (zero, zero))
+        left = residual(field_b, x, (0,), True)[0]
+        for c in range(3):
+            out_ref[c, x - HALO] = field_b[0, c, at(x, 0, True)]
+        return carry + fold(sum(value * value for value in left))
+
+    left_sum = lax.fori_loop(HALO, HALO + ex, squares, zero)
     load_total = jnp.sum(jnp.sum(load_sum, axis=0, keepdims=True), axis=1, keepdims=True)
     left_total = jnp.sum(jnp.sum(left_sum, axis=0, keepdims=True), axis=1, keepdims=True)
     first = lax.broadcasted_iota(jnp.int32, (1, LANES), 1) == 0
@@ -590,8 +631,6 @@
 
     lax.fori_loop(1, total, norm_start, 0)
     norm_recv[total - 1] = mine
-    for copy in out_copies:
-        copy.wait()
     lax.fori_loop(1, total, norm_wait, 0)
 
     def add(device, carry):
@@ -619,12 +658,12 @@
     displacement, norms = pl.pallas_call(
         functools.partial(kernel, counts, (ex, ey, ez)),
         out_shape=(
-            jax.ShapeDtypeStruct(right_side.shape, f32),
-            jax.ShapeDtypeStruct((1, LANES), f32),
+            pltpu.VMEM(right_side.shape, f32),
+            pltpu.VMEM((1, LANES), f32),
         ),
         in_specs=[pl.BlockSpec(memory_space=pl.ANY)] * 2,
         out_specs=(
-            pl.BlockSpec(memory_space=pl.ANY),
+            pl.BlockSpec(memory_space=pltpu.VMEM),
             pl.BlockSpec(memory_space=pltpu.VMEM),
         ),
         scratch_shapes=[
@@ -644,7 +683,8 @@
             vmem((4, LANES), f32),
             vmem((window, counts[0], counts[1], 4, LANES), f32),
             vmem((counts[0] + 2, 3, 8 + coarse_rows, LANES), f32),
-            vmem((2, 3, 3, wide_y, LANES), f32),
+            vmem((2, 3, 9 * rows, LANES), f32),
+            vmem((2, 3, 9 * rows, LANES), f32),
             vmem((1, LANES), f32),
             vmem((total, 1, LANES), f32),
             dma((ex + 1,)),
@@ -654,6 +694,7 @@
             dma((window, counts[0], counts[1])),
             dma((total,)),
             dma((total,)),
+            pltpu.SemaphoreType.REGULAR((8, 2)),
         ],
         compiler_params=pltpu.CompilerParams(collective_id=0, has_side_effects=True),
     )(right_side, damage)

time: 42.4 us -> 40.7 us (0.960)
  local copies, waits for them, and re-layouts: 2.95 us -> 1.26 us
    unnamed x3 -> x1, local copies, waits for them, and re-layouts: 2.44 us -> 0.75 us
where the time goes in v2:
time: 40.7 us; the launch traced here: 40.6 us
  Pallas kernels  38.7 us (95%)
  local copies, waits for them, and re-layouts  1.26 us (3%)
  between operations  0.64 us (2%)
    pallas_call x1, Pallas kernels, on_device(): pl.pallas_call(functools.partial(kernel, counts, (ex, ey, ez)), out_shape...  38.7 us

profile of v2, /device:TPU:0, one launch (start us, length us, event | category | flops | bytes accessed | tf_op | source)
XLA Modules:
  0.0 40.6 jit_solution(6842400691650444180)
XLA Ops:
  0.6 38.7 %shard_map.41 = (f32[3,16,16,128]{3,2,1,0:T(8,128)S(1)}, f32[1,128]{1,0:T(1,128)S(1)}) custom-call(f32[3,16,16,128]{3,2,1,0:T(8,128)} %load_ref.1, s32[16,16,128]{2,1,0:T(8,128)} %damage_ref.1), custom_call_target="tpu_custom_call" | custom-call | tf_op jit(solution)/shard_map/pallas_call | solution.py:658
  39.3 0.7 %copy.5 = f32[3,16,16,128]{3,2,1,0:T(8,128)} copy(f32[3,16,16,128]{3,2,1,0:T(8,128)S(1)} %get-tuple-element.6) | data formatting | bytes 786432
  40.1 0.5 %slice_bitcast_fusion = f32[2]{0:T(128)} fusion(f32[1,128]{1,0:T(1,128)S(1)} %get-tuple-element.5), kind=kLoop, calls=%fused_computation | loop fusion | bytes 16 | tf_op jit(solution)/shard_map/squeeze | solution.py:701

commit v3 on v2

--- a/solution.py
+++ b/solution.py
@@ -33,7 +33,9 @@
             out.append(("y", 0, dy, 0, part))
         for dx in (-1, 1):
             for dy in (-1, 1):
-                out.append(("xy", dx, dy, 0, part))
+                if part == 1:
+                    out.append(("xy", dx, dy, 0, part))
+                out.append(("xyn", dx, dy, 0, part))
         if part == 0:
             for dz in (-1, 1):
                 for dx in (-1, 0, 1):
@@ -61,6 +63,12 @@
     y_recv,
     xy_send,
     xy_recv,
+    xyn_send,
+    xyn_recv,
+    yz_send,
+    yz_recv,
+    xyz_send,
+    xyz_recv,
     z_send,
     z_recv,
     xz_send,
@@ -159,9 +167,16 @@
                         ]
                     for xs in range(2):
                         x0 = 0 if xs == 0 else ex - HALO
-                        xy_send[xs, side, part, f, layer] = base[
-                            0, f, pl.ds(start + x0 * rows, HALO, stride=rows)
-                        ]
+                        if part == 1:
+                            xy_send[xs, side, f, layer] = base[
+                                0, f, pl.ds(start + x0 * rows, HALO, stride=rows)
+                            ]
+                            continue
+                        for which in range(2):
+                            x0 = 2 * which if xs == 0 else ex - 2 - 2 * which
+                            xyn_send[xs, side, which, f, layer] = base[
+                                0, f, pl.ds(start + x0 * rows, 2, stride=rows)
+                            ]
     for f in range(4):
         packed = None
         for k in range(ex):
@@ -169,6 +184,8 @@
             moved = pltpu.roll(row, (8 * k + HALO) % LANES, 1)
             packed = moved if packed is None else jnp.where(lane // 8 == k, moved, packed)
         z_send[f] = packed
+        yz_send[0, f] = packed[:HALO]
+        yz_send[1, f] = packed[ey - HALO :]
     for xs in range(2):
         packed = None
         for f in range(4):
@@ -179,6 +196,8 @@
                 moved = pltpu.roll(row, (8 * k + HALO) % LANES, 1)
                 packed = moved if packed is None else jnp.where(lane // 8 == k, moved, packed)
         xz_send[xs] = packed
+        xyz_send[xs, 0] = packed[:HALO]
+        xyz_send[xs, 1] = packed[ey - HALO :]
 
     pl.semaphore_wait(barrier, levels * count_x * count_y - 1)
 
@@ -204,20 +223,19 @@
         elif kind == "y":
             src, dst = y_send.at[ys, part], y_recv.at[1 - ys, part]
         elif kind == "xy":
-            src, dst = xy_send.at[xs, ys, part], xy_recv.at[1 - xs, 1 - ys, part]
+            src, dst = xy_send.at[xs, ys], xy_recv.at[1 - xs, 1 - ys]
+        elif kind == "xyn":
+            src, dst = xyn_send.at[xs, ys, part], xyn_recv.at[1 - xs, 1 - ys, part]
         else:
-            if dy == 0:
-                src_y, dst_y, size = 0, ypad, ey
-            elif dy < 0:
-                src_y, dst_y, size = 0, ypad + ey, ypad
+            own = pl.ds(ypad, ey)
+            if kind == "z" and dy == 0:
+                src, dst = z_send, z_recv.at[1 - zs, :, own]
+            elif kind == "z":
+                src, dst = yz_send.at[ys], yz_recv.at[1 - zs, 1 - ys]
+            elif dy == 0:
+                src, dst = xz_send.at[xs], xz_recv.at[1 - xs, 1 - zs, own]
             else:
-                src_y, dst_y, size = ey - ypad, 0, ypad
-            if kind == "z":
-                src = z_send.at[:, pl.ds(src_y, size)]
-                dst = z_recv.at[1 - zs, :, pl.ds(dst_y, size)]
-            else:
-                src = xz_send.at[xs, pl.ds(src_y, size)]
-                dst = xz_recv.at[1 - xs, 1 - zs, pl.ds(dst_y, size)]
+                src, dst = xyz_send.at[xs, ys], xyz_recv.at[1 - xs, 1 - zs, 1 - ys]
         copy = pltpu.make_async_remote_copy(
             src_ref=src,
             dst_ref=dst,
@@ -265,7 +283,7 @@
 
     def wait_for(part, send):
         for number, message in enumerate(MESSAGES):
-            far = message[0] in ("y", "xy") and message[4] == 1
+            far = message[0] in ("y", "xy", "xyn") and message[4] == 1
             if send and (message[0] == "x") != (part == 0):
                 continue
             if not send and far != (part == 1):
@@ -292,15 +310,28 @@
                         base[
                             0, f, pl.ds((HALO + 8 * half) * rows + y, 8, stride=rows)
                         ] = y_recv[side, part, f, layer, pl.ds(8 * half, 8)]
+                    near_y = ypad - 2 + layer if side == 0 else ypad + ey + layer
                     for xs in range(2):
                         x0 = 0 if xs == 0 else HALO + ex
-                        base[0, f, pl.ds(x0 * rows + y, HALO, stride=rows)] = xy_recv[
+                        if part == 1:
+                            base[0, f, pl.ds(x0 * rows + y, HALO, stride=rows)] = xy_recv[
+                                xs, side, f, layer
+                            ]
+                        x0 = 2 - 2 * part if xs == 0 else HALO + ex + 2 * part
+                        base[0, f, pl.ds(x0 * rows + near_y, 2, stride=rows)] = xyn_recv[
                             xs, side, part, f, layer
                         ]
 
     def unpack_z():
         lane_rows = lax.broadcasted_iota(jnp.int32, (rows, LANES), 1)
         lower = lax.rem(lane_rows, 8) < HALO
+        for zs in range(2):
+            for ys in range(2):
+                edge = pl.ds(first_y if ys == 0 else ypad + ey, HALO)
+                for f in range(4):
+                    z_recv[zs, f, edge] = yz_recv[zs, ys, f]
+                for xs in range(2):
+                    xz_recv[xs, zs, edge] = xyz_recv[xs, zs, ys]
         for f in range(4):
             merged = jnp.where(lower, z_recv[0, f], z_recv[1, f])
             for k in range(ex):
@@ -674,8 +705,14 @@
             vmem((ex, ey, LANES), jnp.int32),
             vmem((2, 2, 4, 2, ex, LANES), f32),
             vmem((2, 2, 4, 2, ex, LANES), f32),
-            vmem((2, 2, 2, 4, 2, HALO, LANES), f32),
-            vmem((2, 2, 2, 4, 2, HALO, LANES), f32),
+            vmem((2, 2, 4, 2, HALO, LANES), f32),
+            vmem((2, 2, 4, 2, HALO, LANES), f32),
+            vmem((2, 2, 2, 4, 2, 2, LANES), f32),
+            vmem((2, 2, 2, 4, 2, 2, LANES), f32),
+            vmem((2, 4, HALO, LANES), f32),
+            vmem((2, 2, 4, HALO, LANES), f32),
+            vmem((2, 2, HALO, LANES), f32),
+            vmem((2, 2, 2, HALO, LANES), f32),
             vmem((4, ey, LANES), f32),
             vmem((2, 4, rows, LANES), f32),
             vmem((2, ey, LANES), f32),

time: 40.7 us -> 39.9 us (0.980)
  Pallas kernels: 38.7 us -> 37.9 us
    pallas_call x1, Pallas kernels: 38.7 us -> 37.9 us  [on_device(): pl.pallas_call(functools.partial(kernel, counts, (ex, ey, ez)), out_shape...]
where the time goes in v3:
time: 39.9 us; the launch traced here: 39.8 us
  Pallas kernels  37.9 us (95%)
  local copies, waits for them, and re-layouts  1.26 us (3%)
  between operations  0.64 us (2%)
    pallas_call x1, Pallas kernels, on_device(): pl.pallas_call(functools.partial(kernel, counts, (ex, ey, ez)), out_shape...  37.9 us

profile of v3, /device:TPU:0, one launch (start us, length us, event | category | flops | bytes accessed | tf_op | source)
XLA Modules:
  0.0 39.8 jit_solution(16145473576098196476)
XLA Ops:
  0.6 37.9 %shard_map.41 = (f32[3,16,16,128]{3,2,1,0:T(8,128)S(1)}, f32[1,128]{1,0:T(1,128)S(1)}) custom-call(f32[3,16,16,128]{3,2,1,0:T(8,128)} %load_ref.1, s32[16,16,128]{2,1,0:T(8,128)} %damage_ref.1), custom_call_target="tpu_custom_call" | custom-call | tf_op jit(solution)/shard_map/pallas_call | solution.py:689
  38.5 0.7 %copy.5 = f32[3,16,16,128]{3,2,1,0:T(8,128)} copy(f32[3,16,16,128]{3,2,1,0:T(8,128)S(1)} %get-tuple-element.6) | data formatting | bytes 786432
  39.3 0.5 %slice_bitcast_fusion = f32[2]{0:T(128)} fusion(f32[1,128]{1,0:T(1,128)S(1)} %get-tuple-element.5), kind=kLoop, calls=%fused_computation | loop fusion | bytes 16 | tf_op jit(solution)/shard_map/squeeze | solution.py:738

commit v4 on v3

--- a/solution.py
+++ b/solution.py
@@ -45,6 +45,17 @@
 
 
 MESSAGES = messages()
+
+
+def by_two(low, high, body, carry):
+    pairs = (high - low) // 2
+
+    def both(trip, carry):
+        carry = body(low + 2 * trip, carry)
+        return body(low + 2 * trip + 1, carry)
+
+    carry = lax.fori_loop(0, pairs, both, carry)
+    return body(high - 1, carry) if (high - low) % 2 else carry
 
 
 def kernel(
@@ -445,7 +456,7 @@
                     target[t, c, at(x)] = source[t, c, at(x)] + inv * left[t][c]
             return carry
 
-        lax.fori_loop(low, high, one, 0)
+        by_two(low, high, one, 0)
 
     def fold(value):
         return jnp.sum(value.reshape(ey // 8, 8, LANES), axis=0)
@@ -456,7 +467,7 @@
     wait_for(0, True)
     unpack_y(0)
     unpack_z()
-    lax.fori_loop(2, wide_x - 2, prepare, 0)
+    by_two(2, wide_x - 2, prepare, 0)
     sweep(field_a, field_b, 3, wide_x - 3)
 
     def restrict(x, carry):
@@ -465,7 +476,7 @@
         sums.append(carry[3] + fold(base[0, 3, at(x, 0, True)]))
         return tuple(sums)
 
-    sums = lax.fori_loop(HALO, HALO + ex, restrict, (zero,) * 4)
+    sums = by_two(HALO, HALO + ex, restrict, (zero,) * 4)
     stacked = jnp.concatenate([jnp.sum(s, axis=0, keepdims=True) for s in sums] + [zero[:4]], axis=0)
     source_lane = lax.broadcasted_iota(jnp.int32, (LANES, LANES), 0)
     target_lane = lax.broadcasted_iota(jnp.int32, (LANES, LANES), 1)
@@ -498,7 +509,7 @@
 
     wait_for(1, False)
     unpack_y(1)
-    lax.fori_loop(0, wide_x, prepare, 0)
+    by_two(0, wide_x, prepare, 0)
     sweep(field_a, field_b, 1, wide_x - 1)
     sweep(field_b, field_a, 2, wide_x - 2)
 
@@ -506,7 +517,7 @@
         loads = [base[0, c, at(x, 0, True)] for c in range(3)]
         return carry + fold(sum(value * value for value in loads))
 
-    load_sum = lax.fori_loop(HALO, HALO + ex, load_squares, zero)
+    load_sum = by_two(HALO, HALO + ex, load_squares, zero)
     wait_for(1, True)
     for number in range(len(rounds)):
         if number > 0:
@@ -626,7 +637,7 @@
                 )
         return carry
 
-    lax.fori_loop(2, wide_x - 2, correct, 0)
+    by_two(2, wide_x - 2, correct, 0)
     sweep(field_a, field_b, 3, wide_x - 3)
 
     def squares(x, carry):
@@ -635,7 +646,7 @@
             out_ref[c, x - HALO] = field_b[0, c, at(x, 0, True)]
         return carry + fold(sum(value * value for value in left))
 
-    left_sum = lax.fori_loop(HALO, HALO + ex, squares, zero)
+    left_sum = by_two(HALO, HALO + ex, squares, zero)
     load_total = jnp.sum(jnp.sum(load_sum, axis=0, keepdims=True), axis=1, keepdims=True)
     left_total = jnp.sum(jnp.sum(left_sum, axis=0, keepdims=True), axis=1, keepdims=True)
     first = lax.broadcasted_iota(jnp.int32, (1, LANES), 1) == 0

time: 39.9 us -> 35.5 us (0.89)
  Pallas kernels: 37.9 us -> 33.5 us
    pallas_call x1, Pallas kernels: 37.9 us -> 33.5 us  [on_device(): pl.pallas_call(functools.partial(kernel, counts, (ex, ey, ez)), out_shape...]
where the time goes in v4:
time: 35.5 us; the launch traced here: 35.4 us
  Pallas kernels  33.5 us (94%)
  local copies, waits for them, and re-layouts  1.26 us (4%)
  between operations  0.64 us (2%)
    pallas_call x1, Pallas kernels, on_device(): pl.pallas_call(functools.partial(kernel, counts, (ex, ey, ez)), out_shape...  33.5 us
    unnamed x1, local copies, waits for them, and re-layouts  0.75 us

profile of v4, /device:TPU:0, one launch (start us, length us, event | category | flops | bytes accessed | tf_op | source)
XLA Modules:
  0.0 35.4 jit_solution(12997327303901571024)
XLA Ops:
  0.6 33.5 %shard_map.41 = (f32[3,16,16,128]{3,2,1,0:T(8,128)S(1)}, f32[1,128]{1,0:T(1,128)S(1)}) custom-call(f32[3,16,16,128]{3,2,1,0:T(8,128)} %load_ref.1, s32[16,16,128]{2,1,0:T(8,128)} %damage_ref.1), custom_call_target="tpu_custom_call" | custom-call | tf_op jit(solution)/shard_map/pallas_call | solution.py:700
  34.1 0.7 %copy.5 = f32[3,16,16,128]{3,2,1,0:T(8,128)} copy(f32[3,16,16,128]{3,2,1,0:T(8,128)S(1)} %get-tuple-element.6) | data formatting | bytes 786432
  34.9 0.5 %slice_bitcast_fusion = f32[2]{0:T(128)} fusion(f32[1,128]{1,0:T(1,128)S(1)} %get-tuple-element.5), kind=kLoop, calls=%fused_computation | loop fusion | bytes 16 | tf_op jit(solution)/shard_map/squeeze | solution.py:749
